TPU v7x, 32 devices: a whole 2x2x4 slice. The times are simulated.
32 devices in a mesh: patch: 32 (over z, y, x, core).
Axes of the slice: x: 2, y: 2, z: 4, core: 2. Of those that a mesh axis runs over, the one named last changes fastest.
Arguments:
- grid_latent: bfloat16 [131072, 512], P('patch'), may hold values from -6 to 6
- mesh_latent: bfloat16 [10240, 512], P('patch'), may hold values from -6 to 6
- mesh_cotangent: bfloat16 [10240, 512], P('patch'), may hold values from -6 to 6
- grid_rows: int32 [12288], P('patch'), may hold values from 0 to 4095
- mesh_rows: int32 [12288], P('patch'), may hold values from 0 to 319
- counts: int32 [32, 32], P('patch'), may hold values from 1 to 12, as said below
- w1_grid: bfloat16 [512, 512], replicated, may hold values from -0.25 to 0.25
- w1_mesh: bfloat16 [512, 512], replicated, may hold values from -0.25 to 0.25
- bias_one: float32 [512], replicated, may hold values from -3 to 3
- w2: bfloat16 [512, 512], replicated, may hold values from -0.25 to 0.25
Outputs:
- grid_grad: float32 [131072, 512], P('patch')
- mesh_grad: float32 [10240, 512], P('patch')
- w1_grid_grad: float32 [512, 512], replicated
- w1_mesh_grad: float32 [512, 512], replicated
- w2_grad: float32 [512, 512], replicated
- bias_grad: float32 [512], replicated
Inputs may be any that keep to these rules, and one draw needn't show every extreme that they name: counts[p, q] of the 12 slots from patch p to owner q are live, the first ones; every row and every column of counts has at least one entry equal to 12. `grid_rows`: padding slots hold arbitrary rows in range.
All inputs are finite; a program needn't handle non-finite values.
Results may differ from a plain program's by a relative error of at most 0.007.
Values may be sent and summed in bfloat16 or wider, within the bound.
A program may use at most 128 MiB of HBM per device.

v0:
```python
import math

import jax
import jax.numpy as jnp
from jax import lax
from jax.sharding import PartitionSpec as P


def swish_parts(before):
    logistic = jax.nn.sigmoid(before)
    return (before * logistic, logistic * (1.0 + before * (1.0 - logistic)))


def body(
    grid_latent,
    mesh_latent,
    mesh_cotangent,
    grid_rows,
    mesh_rows,
    counts,
    w1_grid,
    w1_mesh,
    bias_one,
    w2,
):
    members = lax.axis_size("patch")
    slot_count = grid_rows.shape[0]
    capacity = slot_count // members
    live_mask = (jnp.arange(capacity, dtype=jnp.int32)[None, :] < counts[0][:, None]).reshape(
        slot_count
    )
    wanted = lax.all_to_all(grid_rows, "patch", split_axis=0, concat_axis=0, tiled=True)
    grid_in = lax.all_to_all(
        jnp.take(grid_latent, wanted, axis=0), "patch", split_axis=0, concat_axis=0, tiled=True
    )
    grid_proj = jnp.dot(grid_in, w1_grid, preferred_element_type=jnp.float32).astype(jnp.bfloat16)
    mesh_in = jnp.take(mesh_latent, mesh_rows, axis=0)
    before = (
        grid_proj.astype(jnp.float32)
        + jnp.dot(mesh_in, w1_mesh, preferred_element_type=jnp.float32)
        + bias_one
    )
    activation, derivative = swish_parts(before)
    hidden = activation.astype(jnp.bfloat16)
    out_grad = jnp.where(
        live_mask[:, None], jnp.take(mesh_cotangent, mesh_rows, axis=0), jnp.zeros((), jnp.bfloat16)
    )
    hid_grad = jnp.dot(out_grad, w2.T, preferred_element_type=jnp.float32)
    pre_grad = (hid_grad * derivative).astype(jnp.bfloat16)
    edge_grid = jnp.dot(pre_grad, w1_grid.T, preferred_element_type=jnp.float32).astype(
        jnp.bfloat16
    )
    returned = lax.all_to_all(edge_grid, "patch", split_axis=0, concat_axis=0, tiled=True)
    grid_part = jnp.dot(grid_in.T, pre_grad, preferred_element_type=jnp.float32)
    grid_grad = jax.ops.segment_sum(
        returned.astype(jnp.float32), wanted, num_segments=grid_latent.shape[0]
    )
    node_sum = jax.ops.segment_sum(
        pre_grad.astype(jnp.float32), mesh_rows, num_segments=mesh_latent.shape[0]
    )
    mesh_grad = jnp.dot(node_sum, w1_mesh.T.astype(jnp.float32), precision=lax.Precision.HIGHEST)
    mesh_part = jnp.dot(mesh_in.T, pre_grad, preferred_element_type=jnp.float32)
    second_part = jnp.dot(hidden.T, out_grad, preferred_element_type=jnp.float32)
    bias_part = jnp.sum(pre_grad.astype(jnp.float32), axis=0)
    totals = lax.psum((grid_part, mesh_part, second_part, bias_part), "patch")
    norm_scale = 1.0 / math.sqrt(members * slot_count)
    return (
        grid_grad,
        mesh_grad,
        totals[0] * norm_scale,
        totals[1] * norm_scale,
        totals[2] * norm_scale,
        totals[3] * norm_scale,
    )


def solution(mesh):
    return jax.shard_map(
        body,
        mesh=mesh,
        in_specs=(
            P("patch", None),
            P("patch", None),
            P("patch", None),
            P("patch"),
            P("patch"),
            P("patch", None),
            P(),
            P(),
            P(),
            P(),
        ),
        out_specs=(P("patch", None), P("patch", None), P(), P(), P(), P()),
        check_vma=False,
    )
```

profile of v0, /device:TPU:0, one launch (start us, length us, event | category | flops | bytes accessed | tf_op | source)
XLA Modules:
  0.0 210.8 jit_solution(12706923728167780505)
XLA Ops:
  7.2 0.9 all_to_all.20
  8.1 14.3 %all_to_all.30 = s32[32,12,1]{1,2,0:T(1,128)S(1)} all-to-all(s32[32,12,1]{1,2,0:T(1,128)S(1)} %bitcast.18), channel_id=1, replica_groups=mesh['patch'=32] {'patch'}, dimensions={0} | all-to-all | bytes 3072 | tf_op jit(solution)/shard_map/all_to_all | solution.py:32
  22.6 4.8 %gather_fusion = bf16[384,512]{1,0:T(8,128)(2,1)S(1)} fusion(bf16[4096,512]{1,0:T(8,128)(2,1)} %param.12, s32[1024]{0:T(1024)S(1)} %pad_clamp_fusion), kind=kCustom, calls=%fused_computation.2 | custom fusion | bytes 787968 | tf_op jit(solution)/shard_map/jit(_take)/gather | solution.py:34
  27.5 0.9 broadcast_select_fusion
  28.5 2.6 %all-to-all-start.1 = ((bf16[32,12,512]{2,1,0:T(8,128)(2,1)}), bf16[32,12,512]{2,1,0:T(8,128)(2,1)S(1)}, u32[]{:S(2)}, u32[]{:S(2)}) async-start(bf16[32,12,512]{2,1,0:T(8,128)(2,1)} %broadcast_select_fusion), calls=%async_computation.1 | async-start | bytes 1048576 | tf_op jit(solution)/shard_map/all_to_all | solution.py:33
  31.1 0.7 compare_select_fusion.2
  31.8 2.1 gather_fusion.2
  33.9 2.1 gather_fusion.1
  36.2 10.5 %all-to-all-done.1 = bf16[32,12,512]{2,1,0:T(8,128)(2,1)S(1)} async-done(((bf16[32,12,512]{2,1,0:T(8,128)(2,1)}), bf16[32,12,512]{2,1,0:T(8,128)(2,1)S(1)}, u32[]{:S(2)}, u32[]{:S(2)}) %all-to-all-start.1) | async-done | bytes 393248 | tf_op jit(solution)/shard_map/all_to_all | solution.py:33
  47.6 1.6 convert_reduce_fusion
  49.2 1.4 fusion.16
  50.7 1.5 fusion.10
  52.2 1.6 fusion.7
  54.2 0.9 all_to_all.25
  55.1 2.9 %all-to-all-start.2 = ((bf16[32,12,512]{2,1,0:T(8,128)(2,1)}), bf16[32,12,512]{2,1,0:T(8,128)(2,1)S(1)}, u32[]{:S(2)}, u32[]{:S(2)}) async-start(bf16[32,12,512]{2,1,0:T(8,128)(2,1)} %all_to_all.25), calls=%async_computation.2 | async-start | bytes 1048576 | tf_op jit(solution)/shard_map/all_to_all | solution.py:53
  58.5 0.7 reduce.7
  59.3 3.0 %scatter_custom_fusion.1 = f32[320,512]{1,0:T(8,128)S(1)} fusion(s32[384]{0:T(512)S(1)} %copy-done.4, bf16[384,512]{1,0:T(8,128)(2,1)S(1)} %get-tuple-element.11, f32[]{:T(128)} %constant.10.clone.1), kind=kCustom, calls=%fused_computation.15 | custom fusion | flops 393216 | bytes 1048580 | tf_op jit(solution)/shard_map/scatter-add | solution.py:58
  62.4 40.9 %psum.31 = f32[512]{0:T(512)S(1)} all-reduce(f32[512]{0:T(512)S(1)} %get-tuple-element.10), channel_id=1, replica_groups=mesh['patch'=32] {'patch'}, use_global_device_ids=true, to_apply=%region_6.8 | all-reduce | flops 512 | bytes 4096 | tf_op jit(solution)/shard_map/psum | solution.py:65
  103.3 0.6 broadcast_multiply_fusion.3
  103.8 1.6 fusion.15
  105.5 6.7 %scatter_custom_fusion = f32[4096,512]{1,0:T(8,128)} fusion(s32[384]{0:T(512)S(1)} %reshape.109, f32[384,512]{1,0:T(8,128)S(1)} %reshape.111, f32[]{:T(128)} %constant.10.clone.1), kind=kCustom, calls=%fused_computation.5 | custom fusion | flops 196608 | bytes 8388612 | tf_op jit(solution)/shard_map/scatter-add | solution.py:55
  112.2 86.4 %all-reduce.3.cloned.1.call-done = (f32[512,512]{1,0:T(8,128)}, f32[512,512]{1,0:T(8,128)}, f32[512,512]{1,0:T(8,128)}) async-done(((f32[512,512]{1,0:T(8,128)}, f32[512,512]{1,0:T(8,128)}, f32[512,512]{1,0:T(8,128)}), (f32[512,512]{1,0:T(8,128)}, f32[512,512]{1,0:T(8,128)}, f32[512,512]{1,0:T(8,128)})) %all-reduce.3.cloned.1.call-update) | async-done | bytes 3145744 | tf_op jit(solution)/shard_map/psum | solution.py:65
  198.6 2.3 %broadcast_multiply_fusion.2 = f32[512,512]{1,0:T(8,128)} fusion(f32[512,512]{1,0:T(8,128)} %get-tuple-element.7), kind=kLoop, calls=%fused_computation.21 | loop fusion | flops 262144 | bytes 2097152 | tf_op jit(solution)/shard_map/mul | solution.py:70
  200.9 3.1 %broadcast_multiply_fusion = (f32[512,512]{1,0:T(8,128)}, f32[512,512]{1,0:T(8,128)}) fusion(f32[512,512]{1,0:T(8,128)} %get-tuple-element.9, f32[512,512]{1,0:T(8,128)} %get-tuple-element.8), kind=kLoop, calls=%fused_computation.19 | loop fusion | flops 524288 | bytes 4194304 | tf_op jit(solution)/shard_map/mul | solution.py:72
  (33 shorter events, 2.5 us)
Async XLA Ops:
  7.2 39.6 %copy-start = (bf16[512,512]{1,0:T(8,128)(2,1)S(1)}, bf16[512,512]{1,0:T(8,128)(2,1)}, u32[]{:S(2)}) copy-start(bf16[512,512]{1,0:T(8,128)(2,1)} %param.18) | copy-start | bytes 1572868
  7.2 29.0 %copy-start.4 = (s32[384]{0:T(512)S(1)}, s32[384]{0:T(512)}, u32[]{:S(2)}) copy-start(s32[384]{0:T(512)} %param.16) | copy-start | bytes 4612
  7.2 24.6 %copy-start.1 = (bf16[320,512]{1,0:T(8,128)(2,1)S(1)}, bf16[320,512]{1,0:T(8,128)(2,1)}, u32[]{:S(2)}) copy-start(bf16[320,512]{1,0:T(8,128)(2,1)} %param.13) | copy-start | bytes 983044
  7.2 26.7 %copy-start.2 = (bf16[320,512]{1,0:T(8,128)(2,1)S(1)}, bf16[320,512]{1,0:T(8,128)(2,1)}, u32[]{:S(2)}) copy-start(bf16[320,512]{1,0:T(8,128)(2,1)} %param.14) | copy-start | bytes 983044
  7.2 28.8 %copy-start.6 = (s32[1,32]{1,0:T(1,128)S(1)}, s32[1,32]{1,0:T(1,128)}, u32[]{:S(2)}) copy-start(s32[1,32]{1,0:T(1,128)} %param.17) | copy-start | bytes 388
  7.2 39.9 %copy-start.3 = (bf16[512,512]{1,0:T(8,128)(2,1)S(1)}, bf16[512,512]{1,0:T(8,128)(2,1)}, u32[]{:S(2)}) copy-start(bf16[512,512]{1,0:T(8,128)(2,1)} %param.19) | copy-start | bytes 1572868
  7.2 39.9 %copy-start.5 = (f32[512]{0:T(512)S(1)}, f32[512]{0:T(512)}, u32[]{:S(2)}) copy-start(f32[512]{0:T(512)} %param.20) | copy-start | bytes 6148
  28.5 18.2 %all-to-all-start.1 = ((bf16[32,12,512]{2,1,0:T(8,128)(2,1)}), bf16[32,12,512]{2,1,0:T(8,128)(2,1)S(1)}, u32[]{:S(2)}, u32[]{:S(2)}) async-start(bf16[32,12,512]{2,1,0:T(8,128)(2,1)} %broadcast_select_fusion), calls=%async_computation.1 | async-start | bytes 1048576 | tf_op jit(solution)/shard_map/all_to_all | solution.py:33
  31.1 167.5 %all-reduce.3.cloned.1.call-start = ((), (), s32[]{:S(2)}) async-start(), calls=%async_computation.3 | async-start | bytes 6291456 | tf_op jit(solution)/shard_map/psum | solution.py:65
  55.1 50.3 %all-to-all-start.2 = ((bf16[32,12,512]{2,1,0:T(8,128)(2,1)}), bf16[32,12,512]{2,1,0:T(8,128)(2,1)S(1)}, u32[]{:S(2)}, u32[]{:S(2)}) async-start(bf16[32,12,512]{2,1,0:T(8,128)(2,1)} %all_to_all.25), calls=%async_computation.2 | async-start | bytes 1048576 | tf_op jit(solution)/shard_map/all_to_all | solution.py:53
Sparse Core Ops, SparseCore 0:
  53.9 144.5 all-reduce.2
where the time goes:
time: 211 us
  waiting for transfers between devices  96.9 us (46%)
  blocking collectives  55.2 us (26%)
  other arithmetic  18.2 us (9%)
  between operations  14.3 us (7%)
  local copies, waits for them, and re-layouts  11.8 us (6%)
  matrix products  8.91 us (4%)
  starting transfers between devices  5.53 us (3%)
    psum x1, waiting for transfers between devices, body(): totals = lax.psum((grid_part, mesh_part, second_part, bias_part), 'patch')  86.4 us
    psum x1, blocking collectives, body(): totals = lax.psum((grid_part, mesh_part, second_part, bias_part), 'patch')  40.9 us
    all_to_all x1, blocking collectives, body(): lax.all_to_all(grid_rows, 'patch', split_axis=0, concat_axis=0, tiled=True)  14.3 us
    all_to_all x1, waiting for transfers between devices, body(): lax.all_to_all(jnp.take(grid_latent, wanted, axis=0), 'patch', split_axis...  10.5 us
    scatter-add x1, other arithmetic, body(): jax.ops.segment_sum(returned.astype(jnp.float32), wanted, num_segments=gr...  6.72 us
    gather x2, local copies, waits for them, and re-layouts, body(): jnp.take(grid_latent, wanted, axis=0)  4.9 us
  transfers between devices with their start and end apart: 3, of which 2 were waited for; matrix products, arithmetic and copies ran while one was open for 9% of the time, Pallas kernels for 0%

commit v1 on v0

v1 whole, which is shorter than its diff:
```python
import functools
import math

import jax
import jax.numpy as jnp
from jax import lax
from jax.experimental import pallas as pl
from jax.experimental.pallas import tpu as pltpu
from jax.sharding import PartitionSpec as P

BF16 = jnp.bfloat16
F32 = jnp.float32
VMEM_LIMIT = 64 * 1024 * 1024 - 1024 * 1024
MIN_ROWS = 16


def dot(a, b):
    return jnp.dot(a, b, preferred_element_type=F32)


def dot_tn(a, b):
    return lax.dot_general(a, b, (((0,), (0,)), ((), ())), preferred_element_type=F32)


def dot_nt(a, b):
    return lax.dot_general(a, b, (((1,), (1,)), ((), ())), preferred_element_type=F32)


def one_hot(hit):
    return jnp.where(hit, 1.0, 0.0).astype(BF16)


def bit_orders(bits):
    rest = list(range(4, bits))
    if bits < 4:
        return [list(range(bits))] * 3
    return [[0, 1, 2, 3] + rest, [0, 2, 3, 1] + rest, [0, 3, 1, 2] + rest]


def main_kernel(
    n,
    cap,
    cpad,
    grid_any,
    mesh_ref,
    cot_ref,
    grows_ref,
    mcol_ref,
    lcol_ref,
    mrow_ref,
    w1g_ref,
    w1m_ref,
    bias_ref,
    w2_ref,
    edge_out,
    rows_out,
    wsum_out,
    bsum_out,
    mgrad_out,
    glat,
    s_msg,
    r_msg,
    r_rows,
    rows2,
    wide,
    gin,
    pre,
    s_pre,
    r_pre,
    s_bias,
    r_bias,
    acc,
    sbuf,
    rbuf,
    abuf,
    glat_sem,
    phase_send,
    phase_recv,
    red_send,
    red_recv,
    ag_send,
    ag_recv,
):
    me = lax.axis_index("patch")
    width = mesh_ref.shape[1]
    slots = n * cpad
    grid_rows_n = glat.shape[0]
    mesh_n = mesh_ref.shape[0]

    load = pltpu.make_async_copy(grid_any, glat, glat_sem)
    load.start()

    barrier = pltpu.get_barrier_semaphore()

    def greet(k, carry):
        pl.semaphore_signal(barrier, inc=1, device_id=(lax.rem(me + k, n),), device_id_type=pl.DeviceIdType.MESH)
        return carry

    lax.fori_loop(1, n, greet, 0)

    mesh_iota = lax.broadcasted_iota(jnp.int32, (slots, mesh_n), 1)
    mesh_in = dot(one_hot(mcol_ref[...] == mesh_iota), mesh_ref[...]).astype(BF16)
    wide[...] = mesh_in.reshape(n, cpad, width)
    s_msg[:, 0] = wide[:, 0:cap, :]
    cot_in = dot(one_hot(lcol_ref[...] == mesh_iota), cot_ref[...]).astype(BF16)
    wide[...] = cot_in.reshape(n, cpad, width)
    s_msg[:, 1] = wide[:, 0:cap, :]

    pl.semaphore_wait(barrier, n - 1)

    def exchange(phase, src, dst, shared=False):
        def send(k, carry):
            partner = lax.rem(me + k, n)
            pltpu.make_async_remote_copy(
                src_ref=src if shared else src.at[partner],
                dst_ref=dst.at[me],
                send_sem=phase_send.at[phase],
                recv_sem=phase_recv.at[phase],
                device_id=(partner,),
                device_id_type=pl.DeviceIdType.MESH,
            ).start()
            return carry

        lax.fori_loop(1, n, send, 0)

    def arrived(phase, dst):
        part = dst.at[pl.ds(0, n - 1)]
        pltpu.make_async_copy(part, part, phase_recv.at[phase]).wait()

    def left(phase, dst):
        part = dst.at[pl.ds(0, n - 1)]
        pltpu.make_async_copy(part, part, phase_send.at[phase]).wait()

    exchange(0, grows_ref, r_rows)
    exchange(1, s_msg, r_msg)
    r_rows[me] = grows_ref[me]
    r_msg[me] = s_msg[me]
    arrived(0, r_rows)

    def flatten(p, carry):
        rows2[pl.ds(p, 1), :] = r_rows[p].astype(F32)
        return carry

    lax.fori_loop(0, n, flatten, 0)
    table = rows2[...]
    lanes = table.shape[1]
    from_patch = jnp.where(
        lax.broadcasted_iota(jnp.int32, (slots, n), 0) // cpad == lax.broadcasted_iota(jnp.int32, (slots, n), 1), 1.0, 0.0
    )
    spread = jnp.dot(from_patch, table, preferred_element_type=F32, precision=lax.Precision.HIGHEST)
    own_lane = lax.broadcasted_iota(jnp.int32, (slots, lanes), 1) == lax.broadcasted_iota(jnp.int32, (slots, lanes), 0) % cpad
    col = jnp.sum(jnp.where(own_lane, spread, 0.0), axis=1, keepdims=True).astype(jnp.int32)
    to_patch = jnp.where(
        lax.broadcasted_iota(jnp.int32, (n, slots), 1) // cpad == lax.broadcasted_iota(jnp.int32, (n, slots), 0), 1.0, 0.0
    )
    spread_t = lax.dot_general(
        table, to_patch, (((0,), (0,)), ((), ())), preferred_element_type=F32, precision=lax.Precision.HIGHEST
    )
    own_sub = lax.broadcasted_iota(jnp.int32, (lanes, slots), 0) == lax.broadcasted_iota(jnp.int32, (lanes, slots), 1) % cpad
    row = jnp.sum(jnp.where(own_sub, spread_t, 0.0), axis=0, keepdims=True).astype(jnp.int32)
    rows_out[...] = jnp.broadcast_to(row, rows_out.shape)

    load.wait()
    step = min(512, grid_rows_n)
    gin[...] = jnp.zeros_like(gin)

    def gather(i, carry):
        base = pl.multiple_of(i * step, step)
        hit = (col - base) == lax.broadcasted_iota(jnp.int32, (slots, step), 1)
        gin[...] += dot(one_hot(hit), glat[pl.ds(base, step), :])
        return carry

    lax.fori_loop(0, grid_rows_n // step, gather, 0)
    grid_in = gin[...].astype(BF16)
    grid_proj = dot(grid_in, w1g_ref[...]).astype(BF16).astype(F32)

    arrived(1, r_msg)
    wide[...] = jnp.zeros_like(wide)
    wide[:, 0:cap, :] = r_msg[:, 1]
    out_grad = wide[...].reshape(slots, width)
    wide[:, 0:cap, :] = r_msg[:, 0]
    mesh_all = wide[...].reshape(slots, width)
    before = grid_proj + dot(mesh_all, w1m_ref[...]) + bias_ref[...]
    logistic = jax.nn.sigmoid(before)
    hidden = (before * logistic).astype(BF16)
    derivative = logistic * (1.0 + before * (1.0 - logistic))
    pre_f = dot_nt(out_grad, w2_ref[...]) * derivative
    pre_grad = pre_f.astype(BF16)
    pre[...] = pre_grad

    acc[0] = dot_tn(grid_in, pre_grad)
    acc[1] = dot_tn(mesh_all, pre_grad)
    acc[2] = dot_tn(hidden, out_grad)

    bits = n.bit_length() - 1
    orders = bit_orders(bits)
    total = acc.shape[1]
    halvings = 0
    while halvings < bits and (total >> (halvings + 1)) >= MIN_ROWS:
        halvings += 1
    base = [0, 0, 0]

    def partner_of(bit):
        b = lax.rem(me // (1 << bit), 2)
        return b, me + (1 - 2 * b) * (1 << bit)

    def red_copy(s, t, src_at, half, off, partner):
        return pltpu.make_async_remote_copy(
            src_ref=sbuf.at[s, pl.ds(src_at, half), :],
            dst_ref=rbuf.at[s, pl.ds(off, half), :],
            send_sem=red_send.at[s, t],
            recv_sem=red_recv.at[s, t],
            device_id=(partner,),
            device_id_type=pl.DeviceIdType.MESH,
        )

    copies = []

    def start_stage(t):
        started = []
        for s in range(3):
            b, partner = partner_of(orders[s][t])
            if t < halvings:
                half = total >> (t + 1)
                off = total - 2 * half
                give = pl.multiple_of(base[s] + (1 - b) * half, MIN_ROWS)
                keep = pl.multiple_of(base[s] + b * half, MIN_ROWS)
                src_at = give
            else:
                half = total >> halvings
                off = total - half + (t - halvings) * half
                give = keep = base[s]
                src_at = total + (t - halvings) * half
            sbuf[s, pl.ds(src_at, half), :] = acc[s, pl.ds(give, half), :].astype(BF16)
            c = red_copy(s, t, src_at, half, off, partner)
            c.start()
            copies.append(c)
            started.append((c, keep, half, off))
            base[s] = keep
        return started

    def finish_stage(t, started):
        for s in range(3):
            c, keep, half, off = started[s]
            c.wait_recv()
            mine = acc[s, pl.ds(keep, half), :]
            if t >= halvings:
                mine = mine.astype(BF16).astype(F32)
            acc[s, pl.ds(keep, half), :] = mine + rbuf[s, pl.ds(off, half), :].astype(F32)

    started = start_stage(0)

    s_bias[...] = jnp.sum(pre_grad.astype(F32), axis=0, keepdims=True)
    wide[...] = pre_grad.reshape(n, cpad, width)
    s_pre[...] = wide[:, 0:cap, :]
    exchange(2, s_pre, r_pre)
    exchange(3, s_bias, r_bias, shared=True)
    r_pre[me] = s_pre[me]
    r_bias[me] = s_bias[...]
    edge_out[...] = dot_nt(pre[...], w1g_ref[...]).astype(BF16)

    for t in range(bits):
        if t > 0:
            started = start_stage(t)
        finish_stage(t, started)

    ag = []
    for s in range(3):
        size = total >> halvings
        abuf[s, pl.ds(base[s], size), :] = acc[s, pl.ds(base[s], size), :].astype(BF16)
    for t in reversed(range(halvings)):
        row_sends = []
        for s in range(3):
            size = total >> (t + 1)
            b, partner = partner_of(orders[s][t])
            c = pltpu.make_async_remote_copy(
                src_ref=abuf.at[s, pl.ds(base[s], size), :],
                dst_ref=abuf.at[s, pl.ds(base[s], size), :],
                send_sem=ag_send.at[s, t],
                recv_sem=ag_recv.at[s, t],
                device_id=(partner,),
                device_id_type=pl.DeviceIdType.MESH,
            )
            c.start()
            row_sends.append(c)
            ag.append(c)
            base[s] = pl.multiple_of(base[s] - b * size, MIN_ROWS)
        if t == halvings - 1:
            arrived(2, r_pre)
            wide[...] = jnp.zeros_like(wide)
            wide[:, 0:cap, :] = r_pre[...]
            back = wide[...].reshape(slots, width)
            hit = mrow_ref[...] == lax.broadcasted_iota(jnp.int32, (mesh_n, slots), 0)
            node = dot(one_hot(hit), back)
            high = node.astype(BF16)
            low = (node - high.astype(F32)).astype(BF16)
            mgrad_out[...] = dot_nt(high, w1m_ref[...]) + dot_nt(low, w1m_ref[...])
            arrived(3, r_bias)
            bsum_out[...] = jnp.sum(r_bias[...], axis=0)
        for c in row_sends:
            c.wait_recv()
    wsum_out[...] = abuf[...]

    for c in copies + ag:
        c.wait_send()
    left(0, r_rows)
    left(1, r_msg)
    left(2, r_pre)
    left(3, r_bias)


def final_kernel(scale, step, rows_ref, edge_ref, wsum_ref, bsum_ref, mgrad_ref, gg, mg, wg, wm, w2g, bg):
    i = pl.program_id(0)
    slots = rows_ref.shape[1]
    hit = (rows_ref[0:1, :] - i * step) == lax.broadcasted_iota(jnp.int32, (step, slots), 0)
    gg[...] = dot(one_hot(hit), edge_ref[...])
    wg[...] = wsum_ref[0].astype(F32) * scale
    wm[...] = wsum_ref[1].astype(F32) * scale
    w2g[...] = wsum_ref[2].astype(F32) * scale

    @pl.when(i == 0)
    def _():
        mg[...] = mgrad_ref[...]
        bg[...] = bsum_ref[...] * scale


def body(n, grid_latent, mesh_latent, mesh_cotangent, grid_rows, mesh_rows, counts, w1_grid, w1_mesh, bias_one, w2):
    slot_count = grid_rows.shape[0]
    cap = slot_count // n
    cpad = -(-cap // 16) * 16
    lanes = -(-cpad // 128) * 128
    width = mesh_latent.shape[1]
    hid = w1_grid.shape[1]
    grid_n = grid_latent.shape[0]
    mesh_n = mesh_latent.shape[0]
    slots = n * cpad
    bits = n.bit_length() - 1

    pad = ((0, 0), (0, cpad - cap))
    mrows = jnp.pad(mesh_rows.reshape(n, cap), pad, constant_values=-1)
    live = jnp.arange(cpad, dtype=jnp.int32)[None, :] < counts[0][:, None]
    lrows = jnp.where(live, mrows, -1)
    grows = jnp.pad(grid_rows.reshape(n, 1, cap), ((0, 0), (0, 0), (0, lanes - cap)), constant_values=-1)

    vm = pl.BlockSpec(memory_space=pltpu.VMEM)
    extra = (max(0, bits - int(math.log2(width // MIN_ROWS))) + 1) * MIN_ROWS
    edge, rows, wsum, bsum, mgrad = pl.pallas_call(
        functools.partial(main_kernel, n, cap, cpad),
        out_shape=(
            jax.ShapeDtypeStruct((slots, width), BF16),
            jax.ShapeDtypeStruct((8, slots), jnp.int32),
            jax.ShapeDtypeStruct((3, width, hid), BF16),
            jax.ShapeDtypeStruct((1, hid), F32),
            jax.ShapeDtypeStruct((mesh_n, width), F32),
        ),
        in_specs=[pl.BlockSpec(memory_space=pl.ANY)] + [vm] * 10,
        out_specs=(vm,) * 5,
        scratch_shapes=[
            pltpu.VMEM((grid_n, width), BF16),
            pltpu.VMEM((n, 2, cap, width), BF16),
            pltpu.VMEM((n, 2, cap, width), BF16),
            pltpu.VMEM((n, 1, lanes), jnp.int32),
            pltpu.VMEM((n, lanes), F32),
            pltpu.VMEM((n, cpad, width), BF16),
            pltpu.VMEM((slots, width), F32),
            pltpu.VMEM((slots, hid), BF16),
            pltpu.VMEM((n, cap, hid), BF16),
            pltpu.VMEM((n, cap, hid), BF16),
            pltpu.VMEM((1, hid), F32),
            pltpu.VMEM((n, 1, hid), F32),
            pltpu.VMEM((3, width, hid), F32),
            pltpu.VMEM((3, width + extra, hid), BF16),
            pltpu.VMEM((3, width + extra, hid), BF16),
            pltpu.VMEM((3, width, hid), BF16),
            pltpu.SemaphoreType.DMA,
            pltpu.SemaphoreType.DMA((4,)),
            pltpu.SemaphoreType.DMA((4,)),
            pltpu.SemaphoreType.DMA((3, bits)),
            pltpu.SemaphoreType.DMA((3, bits)),
            pltpu.SemaphoreType.DMA((3, bits)),
            pltpu.SemaphoreType.DMA((3, bits)),
        ],
        compiler_params=pltpu.CompilerParams(
            collective_id=0, has_side_effects=True, vmem_limit_bytes=VMEM_LIMIT
        ),
    )(
        grid_latent,
        mesh_latent,
        mesh_cotangent,
        grows,
        mrows.reshape(slots, 1),
        lrows.reshape(slots, 1),
        mrows.reshape(1, slots),
        w1_grid,
        w1_mesh,
        bias_one.reshape(1, hid),
        w2,
    )

    step = min(512, grid_n)
    steps = grid_n // step
    part = width // steps
    scale = 1.0 / math.sqrt(n * slot_count)
    whole = lambda *shape: pl.BlockSpec(shape, lambda i: (0,) * len(shape))
    gg, mg, wg, wm, w2g, bg = pl.pallas_call(
        functools.partial(final_kernel, scale, step),
        grid=(steps,),
        out_shape=(
            jax.ShapeDtypeStruct((grid_n, width), F32),
            jax.ShapeDtypeStruct((mesh_n, width), F32),
            jax.ShapeDtypeStruct((width, hid), F32),
            jax.ShapeDtypeStruct((width, hid), F32),
            jax.ShapeDtypeStruct((width, hid), F32),
            jax.ShapeDtypeStruct((1, hid), F32),
        ),
        in_specs=[
            whole(8, slots),
            whole(slots, width),
            pl.BlockSpec((3, part, hid), lambda i: (0, i, 0)),
            whole(1, hid),
            whole(mesh_n, width),
        ],
        out_specs=(
            pl.BlockSpec((step, width), lambda i: (i, 0)),
            whole(mesh_n, width),
            pl.BlockSpec((part, hid), lambda i: (i, 0)),
            pl.BlockSpec((part, hid), lambda i: (i, 0)),
            pl.BlockSpec((part, hid), lambda i: (i, 0)),
            whole(1, hid),
        ),
        compiler_params=pltpu.CompilerParams(vmem_limit_bytes=VMEM_LIMIT),
    )(rows, edge, wsum, bsum, mgrad)
    return gg, mg, wg, wm, w2g, bg.reshape(hid)


def solution(mesh):
    return jax.shard_map(
        functools.partial(body, mesh.shape["patch"]),
        mesh=mesh,
        in_specs=(
            P("patch", None),
            P("patch", None),
            P("patch", None),
            P("patch"),
            P("patch"),
            P("patch", None),
            P(),
            P(),
            P(),
            P(),
        ),
        out_specs=(P("patch", None), P("patch", None), P(), P(), P(), P()),
        check_vma=False,
    )
```

time: 211 us -> 93.2 us (0.44)
  waiting for transfers between devices: 96.9 us -> 0 us
  Pallas kernels: 0 us -> 85.5 us
  blocking collectives: 55.2 us -> 0 us
  other arithmetic: 18.2 us -> 0.73 us
  between operations: 14.3 us -> 0.65 us
  matrix products: 8.91 us -> 0 us
  local copies, waits for them, and re-layouts: 11.8 us -> 4.57 us
  starting transfers between devices: 5.53 us -> 0 us
    psum x1 -> x0, waiting for transfers between devices: 86.4 us -> none  [body(): totals = lax.psum((grid_part, mesh_part, second_part, bias_part), 'patch')]
    pallas_call x0 -> x2, Pallas kernels: none -> 85.5 us  [the longest x1 76.3 us: body(): pl.pallas_call(functools.partial(main_kernel, n, cap, cpad), out_shape=(j...]
    psum x1 -> x0, blocking collectives: 40.9 us -> none  [body(): totals = lax.psum((grid_part, mesh_part, second_part, bias_part), 'patch')]
    all_to_all x1 -> x0, blocking collectives: 14.3 us -> none  [body(): lax.all_to_all(grid_rows, 'patch', split_axis=0, concat_axis=0, tiled=True)]
    all_to_all x2 -> x0, waiting for transfers between devices: 10.5 us -> none  [the longest x1 10.5 us: body(): lax.all_to_all(jnp.take(grid_latent, wanted, axis=0), 'patch', split_axis...]
    scatter-add x2 -> x0, other arithmetic: 9.76 us -> none  [the longest x1 6.72 us: body(): jax.ops.segment_sum(returned.astype(jnp.float32), wanted, num_segments=gr...]
    gather x4 -> x0, local copies, waits for them, and re-layouts: 9.03 us -> none  [the longest x2 4.9 us: body(): jnp.take(grid_latent, wanted, axis=0)]
    dot_general x8 -> x0, matrix products: 8.91 us -> none  [the longest x1 1.63 us: body(): hid_grad = jnp.dot(out_grad, w2.T, preferred_element_type=jnp.float32)]
  transfers between devices with their start and end apart: 3 -> 0, of which waited for: 2 -> 0; matrix products, arithmetic and copies ran while one was open for 9% -> 0% of each run, Pallas kernels for 0% -> 0%
where the time goes in v1:
time: 93.2 us; the launch traced here: 91.5 us
  Pallas kernels  85.5 us (92%)
  local copies, waits for them, and re-layouts  4.57 us (5%)
    pallas_call x1, Pallas kernels, body(): pl.pallas_call(functools.partial(main_kernel, n, cap, cpad), out_shape=(j...  76.3 us
    pallas_call x1, Pallas kernels, body(): pl.pallas_call(functools.partial(final_kernel, scale, step), grid=(steps,...  9.2 us

profile of v1, /device:TPU:0, one launch (start us, length us, event | category | flops | bytes accessed | tf_op | source)
XLA Modules:
  0.0 91.5 jit_solution(11285236856992497737)
XLA Ops:
  0.6 0.8 reshape.34
  1.4 0.6 pad.8.grows_ref
  2.0 0.8 reshape.35
  2.8 0.7 fusion
  3.6 0.7 reshape.38.mrow_ref
  4.2 0.9 reshape.41.mcol_ref
  5.1 0.9 reshape.42.lcol_ref
  5.9 76.3 %shard_map.145 = (bf16[512,512]{1,0:T(8,128)(2,1)}, s32[8,512]{1,0:T(8,128)}, bf16[3,512,512]{2,1,0:T(8,128)(2,1)}, f32[1,512]{1,0:T(1,128)}, f32[320,512]{1,0:T(8,128)}) custom-call(bf16[4096,512]{1,0:T(8,128)(2,1)} %grid_any.1, bf16[320,512]{1,0:T(8,128)(2,1)} %mesh_ref.1, bf16[320,512]{1,0:T(8,128)(2,1)} %cot_ref.1, s32[32,1,128]{2,1,0:T(1,128)} %pad.8.grows_ref, ...), custom_call_target="tpu_custom_call" | custom-call | tf_op jit(solution)/shard_map/pallas_call | solution.py:347
  82.2 9.2 %shard_map.146 = (f32[4096,512]{1,0:T(8,128)}, f32[320,512]{1,0:T(8,128)}, f32[512,512]{1,0:T(8,128)}, f32[512,512]{1,0:T(8,128)}, f32[512,512]{1,0:T(8,128)}, /*index=5*/f32[1,512]{1,0:T(1,128)}) custom-call(s32[8,512]{1,0:T(8,128)} %get-tuple-element.17.rows_ref, bf16[512,512]{1,0:T(8,128)(2,1)} %get-tuple-element.18.edge_ref, ...), custom_call_target="tpu_custom_call" | custom-call | tf_op jit(solution)/shard_map/pallas_call | solution.py:405

commit v2 on v1

--- a/solution.py
+++ b/solution.py
@@ -45,19 +45,23 @@
     mesh_ref,
     cot_ref,
     grows_ref,
-    mcol_ref,
-    lcol_ref,
-    mrow_ref,
-    w1g_ref,
-    w1m_ref,
+    mrows_ref,
+    counts_ref,
+    w1g_any,
+    w1m_any,
     bias_ref,
-    w2_ref,
+    w2_any,
     edge_out,
     rows_out,
     wsum_out,
     bsum_out,
     mgrad_out,
     glat,
+    w1g_ref,
+    w1m_ref,
+    w2_ref,
+    s_rows,
+    mhot,
     s_msg,
     r_msg,
     r_rows,
@@ -74,6 +78,7 @@
     rbuf,
     abuf,
     glat_sem,
+    weight_sem,
     phase_send,
     phase_recv,
     red_send,
@@ -88,7 +93,10 @@
     mesh_n = mesh_ref.shape[0]
 
     load = pltpu.make_async_copy(grid_any, glat, glat_sem)
-    load.start()
+    loads = [
+        pltpu.make_async_copy(src, dst, weight_sem.at[i])
+        for i, (src, dst) in enumerate(((w1g_any, w1g_ref), (w1m_any, w1m_ref), (w2_any, w2_ref)))
+    ]
 
     barrier = pltpu.get_barrier_semaphore()
 
@@ -98,17 +106,65 @@
 
     lax.fori_loop(1, n, greet, 0)
 
+    for c in loads:
+        c.start()
+    load.start()
+
+    lanes = rows2.shape[1]
+    count = grows_ref.shape[1]
+    chunks = width // 128
+    slot_id = lax.broadcasted_iota(jnp.int32, (slots, 1), 0)
+    slot_patch = slot_id // cpad
+    slot_in = slot_id % cpad
+    at = lax.broadcasted_iota(jnp.int32, (n, count), 1) - cap * lax.broadcasted_iota(jnp.int32, (n, count), 0)
+    own_part = (at >= 0) & (at < cap)
+    lane_of = lax.broadcasted_iota(jnp.int32, (count, lanes), 0) % cap == lax.broadcasted_iota(jnp.int32, (count, lanes), 1)
+    lane_of = jnp.where(lane_of, 1.0, 0.0)
+    in_cap = lax.broadcasted_iota(jnp.int32, (n, lanes), 1) < cap
+    from_patch = jnp.where(slot_patch == lax.broadcasted_iota(jnp.int32, (slots, n), 1), 1.0, 0.0)
+    own_lane = lax.broadcasted_iota(jnp.int32, (slots, lanes), 1) == slot_in
+
+    def table_of(ref):
+        spread = jnp.where(own_part, ref[...].astype(F32), 0.0)
+        out = jnp.dot(spread, lane_of, preferred_element_type=F32, precision=lax.Precision.HIGHEST)
+        return jnp.where(in_cap, out, -1.0)
+
+    def column_of(table):
+        spread = jnp.dot(from_patch, table, preferred_element_type=F32, precision=lax.Precision.HIGHEST)
+        return jnp.sum(jnp.where(own_lane, spread, 0.0), axis=1, keepdims=True).astype(jnp.int32)
+
+    rows2[...] = table_of(grows_ref)
+
+    def split(p, carry):
+        s_rows[p] = rows2[pl.ds(p, 1), :].astype(jnp.int32)
+        return carry
+
+    lax.fori_loop(0, n, split, 0)
+    mcol = column_of(table_of(mrows_ref))
+    counted = jnp.where(
+        slot_patch == lax.broadcasted_iota(jnp.int32, (slots, n), 1), counts_ref[...].astype(F32), 0.0
+    )
+    live = slot_in.astype(F32) < jnp.sum(counted, axis=1, keepdims=True)
+    lcol = jnp.where(live, mcol, -1)
     mesh_iota = lax.broadcasted_iota(jnp.int32, (slots, mesh_n), 1)
-    mesh_in = dot(one_hot(mcol_ref[...] == mesh_iota), mesh_ref[...]).astype(BF16)
-    wide[...] = mesh_in.reshape(n, cpad, width)
-    s_msg[:, 0] = wide[:, 0:cap, :]
-    cot_in = dot(one_hot(lcol_ref[...] == mesh_iota), cot_ref[...]).astype(BF16)
-    wide[...] = cot_in.reshape(n, cpad, width)
-    s_msg[:, 1] = wide[:, 0:cap, :]
+    mhot[...] = one_hot(mcol == mesh_iota)
+
+    def pack(ref, first):
+        for j in range(chunks):
+            ref[:, (first + j) * cap : (first + j + 1) * cap, :] = wide[:, 0:cap, j * 128 : (j + 1) * 128]
+
+    def unpack(ref, first):
+        for j in range(chunks):
+            wide[:, 0:cap, j * 128 : (j + 1) * 128] = ref[:, (first + j) * cap : (first + j + 1) * cap, :]
+
+    wide[...] = dot(mhot[...], mesh_ref[...]).astype(BF16).reshape(n, cpad, width)
+    pack(s_msg, 0)
+    wide[...] = dot(one_hot(lcol == mesh_iota), cot_ref[...]).astype(BF16).reshape(n, cpad, width)
+    pack(s_msg, chunks)
 
     pl.semaphore_wait(barrier, n - 1)
 
-    def exchange(phase, src, dst, shared=False):
+    def exchange(phase, src, dst, shared=False, first=1, last=n):
         def send(k, carry):
             partner = lax.rem(me + k, n)
             pltpu.make_async_remote_copy(
@@ -121,7 +177,7 @@
             ).start()
             return carry
 
-        lax.fori_loop(1, n, send, 0)
+        lax.fori_loop(first, last, send, 0)
 
     def arrived(phase, dst):
         part = dst.at[pl.ds(0, n - 1)]
@@ -131,9 +187,9 @@
         part = dst.at[pl.ds(0, n - 1)]
         pltpu.make_async_copy(part, part, phase_send.at[phase]).wait()
 
-    exchange(0, grows_ref, r_rows)
+    exchange(0, s_rows, r_rows)
     exchange(1, s_msg, r_msg)
-    r_rows[me] = grows_ref[me]
+    r_rows[me] = s_rows[me]
     r_msg[me] = s_msg[me]
     arrived(0, r_rows)
 
@@ -143,13 +199,7 @@
 
     lax.fori_loop(0, n, flatten, 0)
     table = rows2[...]
-    lanes = table.shape[1]
-    from_patch = jnp.where(
-        lax.broadcasted_iota(jnp.int32, (slots, n), 0) // cpad == lax.broadcasted_iota(jnp.int32, (slots, n), 1), 1.0, 0.0
-    )
-    spread = jnp.dot(from_patch, table, preferred_element_type=F32, precision=lax.Precision.HIGHEST)
-    own_lane = lax.broadcasted_iota(jnp.int32, (slots, lanes), 1) == lax.broadcasted_iota(jnp.int32, (slots, lanes), 0) % cpad
-    col = jnp.sum(jnp.where(own_lane, spread, 0.0), axis=1, keepdims=True).astype(jnp.int32)
+    col = column_of(table)
     to_patch = jnp.where(
         lax.broadcasted_iota(jnp.int32, (n, slots), 1) // cpad == lax.broadcasted_iota(jnp.int32, (n, slots), 0), 1.0, 0.0
     )
@@ -161,6 +211,8 @@
     rows_out[...] = jnp.broadcast_to(row, rows_out.shape)
 
     load.wait()
+    for c in loads:
+        c.wait()
     step = min(512, grid_rows_n)
     gin[...] = jnp.zeros_like(gin)
 
@@ -176,9 +228,9 @@
 
     arrived(1, r_msg)
     wide[...] = jnp.zeros_like(wide)
-    wide[:, 0:cap, :] = r_msg[:, 1]
+    unpack(r_msg, chunks)
     out_grad = wide[...].reshape(slots, width)
-    wide[:, 0:cap, :] = r_msg[:, 0]
+    unpack(r_msg, 0)
     mesh_all = wide[...].reshape(slots, width)
     before = grid_proj + dot(mesh_all, w1m_ref[...]) + bias_ref[...]
     logistic = jax.nn.sigmoid(before)
@@ -188,9 +240,7 @@
     pre_grad = pre_f.astype(BF16)
     pre[...] = pre_grad
 
-    acc[0] = dot_tn(grid_in, pre_grad)
-    acc[1] = dot_tn(mesh_all, pre_grad)
-    acc[2] = dot_tn(hidden, out_grad)
+    terms = ((grid_in, pre_grad), (mesh_all, pre_grad), (hidden, out_grad))
 
     bits = n.bit_length() - 1
     orders = bit_orders(bits)
@@ -219,6 +269,8 @@
     def start_stage(t):
         started = []
         for s in range(3):
+            if t == 0:
+                acc[s] = dot_tn(*terms[s])
             b, partner = partner_of(orders[s][t])
             if t < halvings:
                 half = total >> (t + 1)
@@ -252,16 +304,18 @@
 
     s_bias[...] = jnp.sum(pre_grad.astype(F32), axis=0, keepdims=True)
     wide[...] = pre_grad.reshape(n, cpad, width)
-    s_pre[...] = wide[:, 0:cap, :]
-    exchange(2, s_pre, r_pre)
+    pack(s_pre, 0)
     exchange(3, s_bias, r_bias, shared=True)
     r_pre[me] = s_pre[me]
     r_bias[me] = s_bias[...]
     edge_out[...] = dot_nt(pre[...], w1g_ref[...]).astype(BF16)
 
+    pieces = bits + 2
+    cuts = [1 + (n - 1) * i // pieces for i in range(pieces + 1)]
     for t in range(bits):
         if t > 0:
             started = start_stage(t)
+        exchange(2, s_pre, r_pre, first=cuts[t], last=cuts[t + 1])
         finish_stage(t, started)
 
     ag = []
@@ -285,13 +339,15 @@
             row_sends.append(c)
             ag.append(c)
             base[s] = pl.multiple_of(base[s] - b * size, MIN_ROWS)
-        if t == halvings - 1:
+        if t >= halvings - 2:
+            i = bits + halvings - 1 - t
+            exchange(2, s_pre, r_pre, first=cuts[i], last=cuts[i + 1])
+        if t == 0:
             arrived(2, r_pre)
             wide[...] = jnp.zeros_like(wide)
-            wide[:, 0:cap, :] = r_pre[...]
+            unpack(r_pre, 0)
             back = wide[...].reshape(slots, width)
-            hit = mrow_ref[...] == lax.broadcasted_iota(jnp.int32, (mesh_n, slots), 0)
-            node = dot(one_hot(hit), back)
+            node = dot_tn(mhot[...], back)
             high = node.astype(BF16)
             low = (node - high.astype(F32)).astype(BF16)
             mgrad_out[...] = dot_nt(high, w1m_ref[...]) + dot_nt(low, w1m_ref[...])
@@ -336,13 +392,9 @@
     slots = n * cpad
     bits = n.bit_length() - 1
 
-    pad = ((0, 0), (0, cpad - cap))
-    mrows = jnp.pad(mesh_rows.reshape(n, cap), pad, constant_values=-1)
-    live = jnp.arange(cpad, dtype=jnp.int32)[None, :] < counts[0][:, None]
-    lrows = jnp.where(live, mrows, -1)
-    grows = jnp.pad(grid_rows.reshape(n, 1, cap), ((0, 0), (0, 0), (0, lanes - cap)), constant_values=-1)
-
     vm = pl.BlockSpec(memory_space=pltpu.VMEM)
+    hbm = pl.BlockSpec(memory_space=pl.ANY)
+    chunks = width // 128
     extra = (max(0, bits - int(math.log2(width // MIN_ROWS))) + 1) * MIN_ROWS
     edge, rows, wsum, bsum, mgrad = pl.pallas_call(
         functools.partial(main_kernel, n, cap, cpad),
@@ -353,19 +405,24 @@
             jax.ShapeDtypeStruct((1, hid), F32),
             jax.ShapeDtypeStruct((mesh_n, width), F32),
         ),
-        in_specs=[pl.BlockSpec(memory_space=pl.ANY)] + [vm] * 10,
+        in_specs=[hbm, vm, vm, vm, vm, vm, hbm, hbm, vm, hbm],
         out_specs=(vm,) * 5,
         scratch_shapes=[
             pltpu.VMEM((grid_n, width), BF16),
-            pltpu.VMEM((n, 2, cap, width), BF16),
-            pltpu.VMEM((n, 2, cap, width), BF16),
+            pltpu.VMEM((width, hid), BF16),
+            pltpu.VMEM((width, hid), BF16),
+            pltpu.VMEM((hid, width), BF16),
+            pltpu.VMEM((n, 1, lanes), jnp.int32),
+            pltpu.VMEM((slots, mesh_n), BF16),
+            pltpu.VMEM((n, 2 * chunks * cap, 128), BF16),
+            pltpu.VMEM((n, 2 * chunks * cap, 128), BF16),
             pltpu.VMEM((n, 1, lanes), jnp.int32),
             pltpu.VMEM((n, lanes), F32),
             pltpu.VMEM((n, cpad, width), BF16),
             pltpu.VMEM((slots, width), F32),
             pltpu.VMEM((slots, hid), BF16),
-            pltpu.VMEM((n, cap, hid), BF16),
-            pltpu.VMEM((n, cap, hid), BF16),
+            pltpu.VMEM((n, chunks * cap, 128), BF16),
+            pltpu.VMEM((n, chunks * cap, 128), BF16),
             pltpu.VMEM((1, hid), F32),
             pltpu.VMEM((n, 1, hid), F32),
             pltpu.VMEM((3, width, hid), F32),
@@ -373,6 +430,7 @@
             pltpu.VMEM((3, width + extra, hid), BF16),
             pltpu.VMEM((3, width, hid), BF16),
             pltpu.SemaphoreType.DMA,
+            pltpu.SemaphoreType.DMA((3,)),
             pltpu.SemaphoreType.DMA((4,)),
             pltpu.SemaphoreType.DMA((4,)),
             pltpu.SemaphoreType.DMA((3, bits)),
@@ -387,10 +445,9 @@
         grid_latent,
         mesh_latent,
         mesh_cotangent,
-        grows,
-        mrows.reshape(slots, 1),
-        lrows.reshape(slots, 1),
-        mrows.reshape(1, slots),
+        grid_rows.reshape(1, slot_count),
+        mesh_rows.reshape(1, slot_count),
+        counts,
         w1_grid,
         w1_mesh,
         bias_one.reshape(1, hid),

time: 93.2 us -> 80.1 us (0.86)
  Pallas kernels: 85.5 us -> 76 us
  local copies, waits for them, and re-layouts: 4.57 us -> 2.49 us
    pallas_call x1, Pallas kernels: 76.3 us -> 66.8 us  [body(): pl.pallas_call(functools.partial(main_kernel, n, cap, cpad), out_shape=(j...]
    reshape x5 -> x2, local copies, waits for them, and re-layouts: 3.94 us -> 2.49 us  [the longest x1 1.25 us: body(): grid_rows.reshape(1, slot_count)]
where the time goes in v2:
time: 80.1 us; the launch traced here: 79.1 us
  Pallas kernels  76 us (95%)
  local copies, waits for them, and re-layouts  2.49 us (3%)
    pallas_call x1, Pallas kernels, body(): pl.pallas_call(functools.partial(main_kernel, n, cap, cpad), out_shape=(j...  66.8 us
    pallas_call x1, Pallas kernels, body(): pl.pallas_call(functools.partial(final_kernel, scale, step), grid=(steps,...  9.2 us

profile of v2, /device:TPU:0, one launch (start us, length us, event | category | flops | bytes accessed | tf_op | source)
XLA Modules:
  0.0 79.1 jit_solution(177433095445651773)
XLA Ops:
  0.6 1.2 %reshape.24.grows_ref = s32[1,384]{1,0:T(1,128)} reshape(s32[384]{0:T(512)} %param.13) | data formatting | bytes 3072 | tf_op jit(solution)/shard_map/reshape | solution.py:448
  1.9 1.2 %reshape.25.mrows_ref = s32[1,384]{1,0:T(1,128)} reshape(s32[384]{0:T(512)} %param.14) | data formatting | bytes 3072 | tf_op jit(solution)/shard_map/reshape | solution.py:449
  3.1 66.8 %shard_map.145 = (bf16[512,512]{1,0:T(8,128)(2,1)}, s32[8,512]{1,0:T(8,128)}, bf16[3,512,512]{2,1,0:T(8,128)(2,1)}, f32[1,512]{1,0:T(1,128)}, f32[320,512]{1,0:T(8,128)}) custom-call(bf16[4096,512]{1,0:T(8,128)(2,1)} %grid_any.1, bf16[320,512]{1,0:T(8,128)(2,1)} %mesh_ref.1, bf16[320,512]{1,0:T(8,128)(2,1)} %cot_ref.1, s32[1,384]{1,0:T(1,128)} %reshape.24.grows_ref, ...), custom_call_target="tpu_custom_call" | custom-call | tf_op jit(solution)/shard_map/pallas_call | solution.py:399
  69.9 9.2 %shard_map.146 = (f32[4096,512]{1,0:T(8,128)}, f32[320,512]{1,0:T(8,128)}, f32[512,512]{1,0:T(8,128)}, f32[512,512]{1,0:T(8,128)}, f32[512,512]{1,0:T(8,128)}, /*index=5*/f32[1,512]{1,0:T(1,128)}) custom-call(s32[8,512]{1,0:T(8,128)} %get-tuple-element.17.rows_ref, bf16[512,512]{1,0:T(8,128)(2,1)} %get-tuple-element.18.edge_ref, ...), custom_call_target="tpu_custom_call" | custom-call | tf_op jit(solution)/shard_map/pallas_call | solution.py:462

commit v3 on v2

--- a/solution.py
+++ b/solution.py
@@ -31,10 +31,10 @@
 
 
 def bit_orders(bits):
+    if bits < 4:
+        return [list(range(bits))] * 6
     rest = list(range(4, bits))
-    if bits < 4:
-        return [list(range(bits))] * 3
-    return [[0, 1, 2, 3] + rest, [0, 2, 3, 1] + rest, [0, 3, 1, 2] + rest]
+    return [[0, *order, *rest] for order in ((1, 2, 3), (2, 3, 1), (3, 1, 2), (1, 3, 2), (2, 1, 3), (3, 2, 1))]
 
 
 def main_kernel(
@@ -111,7 +111,7 @@
     load.start()
 
     lanes = rows2.shape[1]
-    count = grows_ref.shape[1]
+    count = grows_ref.shape[0]
     chunks = width // 128
     slot_id = lax.broadcasted_iota(jnp.int32, (slots, 1), 0)
     slot_patch = slot_id // cpad
@@ -125,7 +125,7 @@
     own_lane = lax.broadcasted_iota(jnp.int32, (slots, lanes), 1) == slot_in
 
     def table_of(ref):
-        spread = jnp.where(own_part, ref[...].astype(F32), 0.0)
+        spread = jnp.where(own_part, ref[...].reshape(1, count).astype(F32), 0.0)
         out = jnp.dot(spread, lane_of, preferred_element_type=F32, precision=lax.Precision.HIGHEST)
         return jnp.where(in_cap, out, -1.0)
 
@@ -248,7 +248,7 @@
     halvings = 0
     while halvings < bits and (total >> (halvings + 1)) >= MIN_ROWS:
         halvings += 1
-    base = [0, 0, 0]
+    base = [0] * 6
 
     def partner_of(bit):
         b = lax.rem(me // (1 << bit), 2)
@@ -268,9 +268,11 @@
 
     def start_stage(t):
         started = []
-        for s in range(3):
-            if t == 0:
-                acc[s] = dot_tn(*terms[s])
+        for s in range(6):
+            if t == 0 and s < 3:
+                term = dot_tn(*terms[s])
+                acc[s] = term[:, : term.shape[1] // 2]
+                acc[s + 3] = term[:, term.shape[1] // 2 :]
             b, partner = partner_of(orders[s][t])
             if t < halvings:
                 half = total >> (t + 1)
@@ -292,7 +294,7 @@
         return started
 
     def finish_stage(t, started):
-        for s in range(3):
+        for s in range(6):
             c, keep, half, off = started[s]
             c.wait_recv()
             mine = acc[s, pl.ds(keep, half), :]
@@ -319,12 +321,12 @@
         finish_stage(t, started)
 
     ag = []
-    for s in range(3):
+    for s in range(6):
         size = total >> halvings
         abuf[s, pl.ds(base[s], size), :] = acc[s, pl.ds(base[s], size), :].astype(BF16)
     for t in reversed(range(halvings)):
         row_sends = []
-        for s in range(3):
+        for s in range(6):
             size = total >> (t + 1)
             b, partner = partner_of(orders[s][t])
             c = pltpu.make_async_remote_copy(
@@ -355,7 +357,9 @@
             bsum_out[...] = jnp.sum(r_bias[...], axis=0)
         for c in row_sends:
             c.wait_recv()
-    wsum_out[...] = abuf[...]
+    for s in range(3):
+        wsum_out[s, :, : abuf.shape[2]] = abuf[s]
+        wsum_out[s, :, abuf.shape[2] :] = abuf[s + 3]
 
     for c in copies + ag:
         c.wait_send()
@@ -365,19 +369,31 @@
     left(3, r_bias)
 
 
-def final_kernel(scale, step, rows_ref, edge_ref, wsum_ref, bsum_ref, mgrad_ref, gg, mg, wg, wm, w2g, bg):
-    i = pl.program_id(0)
+def final_kernel(
+    scale, step, rows_ref, edge_ref, bsum_ref, mgrad_ref, wsum_any, gg, mg, wg, wm, w2g, bg, gbuf, wsum, wbuf, sems
+):
     slots = rows_ref.shape[1]
-    hit = (rows_ref[0:1, :] - i * step) == lax.broadcasted_iota(jnp.int32, (step, slots), 0)
-    gg[...] = dot(one_hot(hit), edge_ref[...])
-    wg[...] = wsum_ref[0].astype(F32) * scale
-    wm[...] = wsum_ref[1].astype(F32) * scale
-    w2g[...] = wsum_ref[2].astype(F32) * scale
-
-    @pl.when(i == 0)
-    def _():
-        mg[...] = mgrad_ref[...]
-        bg[...] = bsum_ref[...] * scale
+    steps = gbuf.shape[0] // step
+    load = pltpu.make_async_copy(wsum_any, wsum, sems.at[0])
+    load.start()
+    copies = [pltpu.make_async_copy(mgrad_ref, mg, sems.at[1])]
+    copies[0].start()
+    for i in range(steps):
+        part = pl.ds(i * step, step)
+        hit = (rows_ref[0:1, :] - i * step) == lax.broadcasted_iota(jnp.int32, (step, slots), 0)
+        gbuf[part, :] = dot(one_hot(hit), edge_ref[...])
+        c = pltpu.make_async_copy(gbuf.at[part, :], gg.at[part, :], sems.at[5 + i])
+        c.start()
+        copies.append(c)
+    load.wait()
+    for s, out in enumerate((wg, wm, w2g)):
+        wbuf[s] = wsum[s].astype(F32) * scale
+        c = pltpu.make_async_copy(wbuf.at[s], out, sems.at[2 + s])
+        c.start()
+        copies.append(c)
+    bg[...] = bsum_ref[...] * scale
+    for c in copies:
+        c.wait()
 
 
 def body(n, grid_latent, mesh_latent, mesh_cotangent, grid_rows, mesh_rows, counts, w1_grid, w1_mesh, bias_one, w2):
@@ -425,18 +441,18 @@
             pltpu.VMEM((n, chunks * cap, 128), BF16),
             pltpu.VMEM((1, hid), F32),
             pltpu.VMEM((n, 1, hid), F32),
-            pltpu.VMEM((3, width, hid), F32),
-            pltpu.VMEM((3, width + extra, hid), BF16),
-            pltpu.VMEM((3, width + extra, hid), BF16),
-            pltpu.VMEM((3, width, hid), BF16),
+            pltpu.VMEM((6, width, hid // 2), F32),
+            pltpu.VMEM((6, width + extra, hid // 2), BF16),
+            pltpu.VMEM((6, width + extra, hid // 2), BF16),
+            pltpu.VMEM((6, width, hid // 2), BF16),
             pltpu.SemaphoreType.DMA,
             pltpu.SemaphoreType.DMA((3,)),
             pltpu.SemaphoreType.DMA((4,)),
             pltpu.SemaphoreType.DMA((4,)),
-            pltpu.SemaphoreType.DMA((3, bits)),
-            pltpu.SemaphoreType.DMA((3, bits)),
-            pltpu.SemaphoreType.DMA((3, bits)),
-            pltpu.SemaphoreType.DMA((3, bits)),
+            pltpu.SemaphoreType.DMA((6, bits)),
+            pltpu.SemaphoreType.DMA((6, bits)),
+            pltpu.SemaphoreType.DMA((6, bits)),
+            pltpu.SemaphoreType.DMA((6, bits)),
         ],
         compiler_params=pltpu.CompilerParams(
             collective_id=0, has_side_effects=True, vmem_limit_bytes=VMEM_LIMIT
@@ -445,8 +461,8 @@
         grid_latent,
         mesh_latent,
         mesh_cotangent,
-        grid_rows.reshape(1, slot_count),
-        mesh_rows.reshape(1, slot_count),
+        grid_rows,
+        mesh_rows,
         counts,
         w1_grid,
         w1_mesh,
@@ -456,12 +472,9 @@
 
     step = min(512, grid_n)
     steps = grid_n // step
-    part = width // steps
     scale = 1.0 / math.sqrt(n * slot_count)
-    whole = lambda *shape: pl.BlockSpec(shape, lambda i: (0,) * len(shape))
     gg, mg, wg, wm, w2g, bg = pl.pallas_call(
         functools.partial(final_kernel, scale, step),
-        grid=(steps,),
         out_shape=(
             jax.ShapeDtypeStruct((grid_n, width), F32),
             jax.ShapeDtypeStruct((mesh_n, width), F32),
@@ -470,23 +483,16 @@
             jax.ShapeDtypeStruct((width, hid), F32),
             jax.ShapeDtypeStruct((1, hid), F32),
         ),
-        in_specs=[
-            whole(8, slots),
-            whole(slots, width),
-            pl.BlockSpec((3, part, hid), lambda i: (0, i, 0)),
-            whole(1, hid),
-            whole(mesh_n, width),
+        in_specs=[vm, vm, vm, vm, hbm],
+        out_specs=(hbm, hbm, hbm, hbm, hbm, vm),
+        scratch_shapes=[
+            pltpu.VMEM((grid_n, width), F32),
+            pltpu.VMEM((3, width, hid), BF16),
+            pltpu.VMEM((3, width, hid), F32),
+            pltpu.SemaphoreType.DMA((5 + steps,)),
         ],
-        out_specs=(
-            pl.BlockSpec((step, width), lambda i: (i, 0)),
-            whole(mesh_n, width),
-            pl.BlockSpec((part, hid), lambda i: (i, 0)),
-            pl.BlockSpec((part, hid), lambda i: (i, 0)),
-            pl.BlockSpec((part, hid), lambda i: (i, 0)),
-            whole(1, hid),
-        ),
         compiler_params=pltpu.CompilerParams(vmem_limit_bytes=VMEM_LIMIT),
-    )(rows, edge, wsum, bsum, mgrad)
+    )(rows, edge, bsum, mgrad, wsum)
     return gg, mg, wg, wm, w2g, bg.reshape(hid)
 
 

time: 80.1 us -> 75.6 us (0.944)
  local copies, waits for them, and re-layouts: 2.49 us -> 0 us
  Pallas kernels: 76 us -> 74.6 us
    pallas_call x1, Pallas kernels: 9.2 us -> 6.64 us  [body(): pl.pallas_call(functools.partial(final_kernel, scale, step), out_shape=(j...]
    reshape x2 -> x0, local copies, waits for them, and re-layouts: 2.49 us -> none  [the longest x1 1.25 us: body(): grid_rows.reshape(1, slot_count)]
    pallas_call x1, Pallas kernels: 66.8 us -> 67.9 us  [body(): pl.pallas_call(functools.partial(main_kernel, n, cap, cpad), out_shape=(j...]
where the time goes in v3:
time: 75.6 us; the launch traced here: 75.2 us
  Pallas kernels  74.6 us (99%)
    pallas_call x1, Pallas kernels, body(): pl.pallas_call(functools.partial(main_kernel, n, cap, cpad), out_shape=(j...  67.9 us
    pallas_call x1, Pallas kernels, body(): pl.pallas_call(functools.partial(final_kernel, scale, step), out_shape=(j...  6.64 us

profile of v3, /device:TPU:0, one launch (start us, length us, event | category | flops | bytes accessed | tf_op | source)
XLA Modules:
  0.0 75.2 jit_solution(10735526457159272017)
XLA Ops:
  0.6 67.9 %shard_map.145 = (bf16[512,512]{1,0:T(8,128)(2,1)}, s32[8,512]{1,0:T(8,128)}, bf16[3,512,512]{2,1,0:T(8,128)(2,1)}, f32[1,512]{1,0:T(1,128)}, f32[320,512]{1,0:T(8,128)}) custom-call(bf16[4096,512]{1,0:T(8,128)(2,1)} %grid_any.1, bf16[320,512]{1,0:T(8,128)(2,1)} %mesh_ref.1, bf16[320,512]{1,0:T(8,128)(2,1)} %cot_ref.1, s32[384]{0:T(512)} %grows_ref.1, ...), custom_call_target="tpu_custom_call" | custom-call | tf_op jit(solution)/shard_map/pallas_call | solution.py:415
  68.6 6.6 %shard_map.146 = (f32[4096,512]{1,0:T(8,128)}, f32[320,512]{1,0:T(8,128)}, f32[512,512]{1,0:T(8,128)}, f32[512,512]{1,0:T(8,128)}, f32[512,512]{1,0:T(8,128)}, /*index=5*/f32[1,512]{1,0:T(1,128)}) custom-call(s32[8,512]{1,0:T(8,128)} %get-tuple-element.17.rows_ref, bf16[512,512]{1,0:T(8,128)(2,1)} %get-tuple-element.18.edge_ref, ...), custom_call_target="tpu_custom_call" | custom-call | tf_op jit(solution)/shard_map/pallas_call | solution.py:476

commit v4 on v3

--- a/solution.py
+++ b/solution.py
@@ -32,9 +32,9 @@
 
 def bit_orders(bits):
     if bits < 4:
-        return [list(range(bits))] * 6
+        return [list(range(bits))] * 3
     rest = list(range(4, bits))
-    return [[0, *order, *rest] for order in ((1, 2, 3), (2, 3, 1), (3, 1, 2), (1, 3, 2), (2, 1, 3), (3, 2, 1))]
+    return [[0, *order, *rest] for order in ((1, 2, 3), (2, 3, 1), (3, 1, 2))]
 
 
 def main_kernel(
@@ -77,6 +77,9 @@
     sbuf,
     rbuf,
     abuf,
+    edge_buf,
+    mgrad_buf,
+    out_sem,
     glat_sem,
     weight_sem,
     phase_send,
@@ -248,7 +251,7 @@
     halvings = 0
     while halvings < bits and (total >> (halvings + 1)) >= MIN_ROWS:
         halvings += 1
-    base = [0] * 6
+    base = [0] * 3
 
     def partner_of(bit):
         b = lax.rem(me // (1 << bit), 2)
@@ -268,11 +271,9 @@
 
     def start_stage(t):
         started = []
-        for s in range(6):
-            if t == 0 and s < 3:
-                term = dot_tn(*terms[s])
-                acc[s] = term[:, : term.shape[1] // 2]
-                acc[s + 3] = term[:, term.shape[1] // 2 :]
+        for s in range(3):
+            if t == 0:
+                acc[s] = dot_tn(*terms[s])
             b, partner = partner_of(orders[s][t])
             if t < halvings:
                 half = total >> (t + 1)
@@ -294,7 +295,7 @@
         return started
 
     def finish_stage(t, started):
-        for s in range(6):
+        for s in range(3):
             c, keep, half, off = started[s]
             c.wait_recv()
             mine = acc[s, pl.ds(keep, half), :]
@@ -310,7 +311,9 @@
     exchange(3, s_bias, r_bias, shared=True)
     r_pre[me] = s_pre[me]
     r_bias[me] = s_bias[...]
-    edge_out[...] = dot_nt(pre[...], w1g_ref[...]).astype(BF16)
+    edge_buf[...] = dot_nt(pre[...], w1g_ref[...]).astype(BF16)
+    outs = [pltpu.make_async_copy(edge_buf, edge_out, out_sem.at[0])]
+    outs[0].start()
 
     pieces = bits + 2
     cuts = [1 + (n - 1) * i // pieces for i in range(pieces + 1)]
@@ -321,12 +324,12 @@
         finish_stage(t, started)
 
     ag = []
-    for s in range(6):
+    for s in range(3):
         size = total >> halvings
         abuf[s, pl.ds(base[s], size), :] = acc[s, pl.ds(base[s], size), :].astype(BF16)
     for t in reversed(range(halvings)):
         row_sends = []
-        for s in range(6):
+        for s in range(3):
             size = total >> (t + 1)
             b, partner = partner_of(orders[s][t])
             c = pltpu.make_async_remote_copy(
@@ -352,14 +355,15 @@
             node = dot_tn(mhot[...], back)
             high = node.astype(BF16)
             low = (node - high.astype(F32)).astype(BF16)
-            mgrad_out[...] = dot_nt(high, w1m_ref[...]) + dot_nt(low, w1m_ref[...])
+            mgrad_buf[...] = dot_nt(high, w1m_ref[...]) + dot_nt(low, w1m_ref[...])
+            outs.append(pltpu.make_async_copy(mgrad_buf, mgrad_out, out_sem.at[1]))
+            outs[1].start()
             arrived(3, r_bias)
             bsum_out[...] = jnp.sum(r_bias[...], axis=0)
         for c in row_sends:
             c.wait_recv()
-    for s in range(3):
-        wsum_out[s, :, : abuf.shape[2]] = abuf[s]
-        wsum_out[s, :, abuf.shape[2] :] = abuf[s + 3]
+    outs.append(pltpu.make_async_copy(abuf, wsum_out, out_sem.at[2]))
+    outs[2].start()
 
     for c in copies + ag:
         c.wait_send()
@@ -367,6 +371,8 @@
     left(1, r_msg)
     left(2, r_pre)
     left(3, r_bias)
+    for c in outs:
+        c.wait()
 
 
 def final_kernel(
@@ -422,7 +428,7 @@
             jax.ShapeDtypeStruct((mesh_n, width), F32),
         ),
         in_specs=[hbm, vm, vm, vm, vm, vm, hbm, hbm, vm, hbm],
-        out_specs=(vm,) * 5,
+        out_specs=(hbm, vm, hbm, vm, hbm),
         scratch_shapes=[
             pltpu.VMEM((grid_n, width), BF16),
             pltpu.VMEM((width, hid), BF16),
@@ -441,18 +447,21 @@
             pltpu.VMEM((n, chunks * cap, 128), BF16),
             pltpu.VMEM((1, hid), F32),
             pltpu.VMEM((n, 1, hid), F32),
-            pltpu.VMEM((6, width, hid // 2), F32),
-            pltpu.VMEM((6, width + extra, hid // 2), BF16),
-            pltpu.VMEM((6, width + extra, hid // 2), BF16),
-            pltpu.VMEM((6, width, hid // 2), BF16),
+            pltpu.VMEM((3, width, hid), F32),
+            pltpu.VMEM((3, width + extra, hid), BF16),
+            pltpu.VMEM((3, width + extra, hid), BF16),
+            pltpu.VMEM((3, width, hid), BF16),
+            pltpu.VMEM((slots, width), BF16),
+            pltpu.VMEM((mesh_n, width), F32),
+            pltpu.SemaphoreType.DMA((3,)),
             pltpu.SemaphoreType.DMA,
             pltpu.SemaphoreType.DMA((3,)),
             pltpu.SemaphoreType.DMA((4,)),
             pltpu.SemaphoreType.DMA((4,)),
-            pltpu.SemaphoreType.DMA((6, bits)),
-            pltpu.SemaphoreType.DMA((6, bits)),
-            pltpu.SemaphoreType.DMA((6, bits)),
-            pltpu.SemaphoreType.DMA((6, bits)),
+            pltpu.SemaphoreType.DMA((3, bits)),
+            pltpu.SemaphoreType.DMA((3, bits)),
+            pltpu.SemaphoreType.DMA((3, bits)),
+            pltpu.SemaphoreType.DMA((3, bits)),
         ],
         compiler_params=pltpu.CompilerParams(
             collective_id=0, has_side_effects=True, vmem_limit_bytes=VMEM_LIMIT

time: 75.6 us -> 74.8 us (0.989); the launches traced: 75.2 us -> 73.6 us
  Pallas kernels: 74.6 us -> 72.9 us
    pallas_call x1, Pallas kernels: 67.9 us -> 66.3 us  [body(): pl.pallas_call(functools.partial(main_kernel, n, cap, cpad), out_shape=(j...]
where the time goes in v4:
time: 74.8 us; the launch traced here: 73.6 us
  Pallas kernels  72.9 us (97%)
    pallas_call x1, Pallas kernels, body(): pl.pallas_call(functools.partial(main_kernel, n, cap, cpad), out_shape=(j...  66.3 us
    pallas_call x1, Pallas kernels, body(): pl.pallas_call(functools.partial(final_kernel, scale, step), out_shape=(j...  6.64 us

profile of v4, /device:TPU:0, one launch (start us, length us, event | category | flops | bytes accessed | tf_op | source)
XLA Modules:
  0.0 73.6 jit_solution(877846358073906483)
XLA Ops:
  0.6 66.3 %shard_map.145 = (bf16[512,512]{1,0:T(8,128)(2,1)}, s32[8,512]{1,0:T(8,128)}, bf16[3,512,512]{2,1,0:T(8,128)(2,1)}, f32[1,512]{1,0:T(1,128)}, f32[320,512]{1,0:T(8,128)}) custom-call(bf16[4096,512]{1,0:T(8,128)(2,1)} %grid_any.1, bf16[320,512]{1,0:T(8,128)(2,1)} %mesh_ref.1, bf16[320,512]{1,0:T(8,128)(2,1)} %cot_ref.1, s32[384]{0:T(512)} %grows_ref.1, ...), custom_call_target="tpu_custom_call" | custom-call | tf_op jit(solution)/shard_map/pallas_call | solution.py:421
  66.9 6.6 %shard_map.146 = (f32[4096,512]{1,0:T(8,128)}, f32[320,512]{1,0:T(8,128)}, f32[512,512]{1,0:T(8,128)}, f32[512,512]{1,0:T(8,128)}, f32[512,512]{1,0:T(8,128)}, /*index=5*/f32[1,512]{1,0:T(1,128)}) custom-call(s32[8,512]{1,0:T(8,128)} %get-tuple-element.17.rows_ref, bf16[512,512]{1,0:T(8,128)(2,1)} %get-tuple-element.18.edge_ref, ...), custom_call_target="tpu_custom_call" | custom-call | tf_op jit(solution)/shard_map/pallas_call | solution.py:485
